TPU v7x, 32 devices: a whole 2x2x4 slice. The times are simulated.
32 devices in a mesh: dp: 8 (over z, core), tensor: 4 (over y, x).
Axes of the slice: x: 2, y: 2, z: 4, core: 2. Of those that a mesh axis runs over, the one named last changes fastest.
Arguments:
- block_input: bfloat16 [8192, 2048], P(('dp', 'tensor')), may hold values from -6 to 6
- attention_gain: float32 [2048], replicated, may hold values from 0.1 to 1.9
- query_weight: bfloat16 [2048, 2048], P('dp', 'tensor'), may hold values from -0.125 to 0.125
- key_matrix: bfloat16 [2048, 1024], P('dp', 'tensor'), may hold values from -0.125 to 0.125
- value_matrix: bfloat16 [2048, 1024], P('dp', 'tensor'), may hold values from -0.125 to 0.125
- query_gain: float32 [128], replicated, may hold values from 0.4 to 2
- key_gain: float32 [128], replicated, may hold values from 0.4 to 2
- output_weight: bfloat16 [2048, 2048], P('tensor', 'dp'), may hold values from -1 to 1
- feed_gain: float32 [2048], replicated, may hold values from 0.1 to 1.9
- gate_weight: bfloat16 [2048, 6144], P('dp', 'tensor'), may hold values from -0.125 to 0.125
- up_weight: bfloat16 [2048, 6144], P('dp', 'tensor'), may hold values from -0.125 to 0.125
- down_weight: bfloat16 [6144, 2048], P('tensor', 'dp'), may hold values from -0.078125 to 0.078125
- out_cotangent: bfloat16 [8192, 2048], P(('dp', 'tensor')), may hold values from -6 to 6
Outputs:
- block_output: bfloat16 [8192, 2048], P(('dp', 'tensor'))
- input_gradient: bfloat16 [8192, 2048], P(('dp', 'tensor'))
- attention_gain_gradient: float32 [2048], replicated
- query_gradient: float32 [2048, 2048], P('dp', 'tensor')
- key_gradient: float32 [2048, 1024], P('dp', 'tensor')
- value_gradient: float32 [2048, 1024], P('dp', 'tensor')
- query_gain_gradient: float32 [128], replicated
- key_gain_gradient: float32 [128], replicated
- output_gradient: float32 [2048, 2048], P('tensor', 'dp')
- feed_gain_gradient: float32 [2048], replicated
- gate_gradient: float32 [2048, 6144], P('dp', 'tensor')
- up_gradient: float32 [2048, 6144], P('dp', 'tensor')
- down_gradient: float32 [6144, 2048], P('tensor', 'dp')
All inputs are finite; a program needn't handle non-finite values.
Results may differ from a plain program's by a relative error of at most 0.019.
Values may be sent and summed in bfloat16 or wider, within the bound.
A program may use at most 256 MiB of HBM per device.

v0:
```python
import jax
import jax.numpy as jnp
from jax import lax
from jax.sharding import PartitionSpec as P

SEQUENCE_LENGTH = 1024
epsilon = 1e-06
rope_base = 1000000.0


def row_scale(values):
    return lax.rsqrt(jnp.mean(values * values, axis=-1, keepdims=True) + epsilon)


def rotate_half(values):
    half_size = values.shape[-1] // 2
    return jnp.concatenate([-values[..., half_size:], values[..., :half_size]], axis=-1)


def rope_tables(positions, head_size):
    half_size = head_size // 2
    frequency = rope_base ** (-(jnp.arange(half_size).astype(jnp.float32) * 2.0 / head_size))
    angles = positions[:, None] * frequency[None, :]
    angles = jnp.concatenate([angles, angles], axis=1)
    return (jnp.cos(angles)[:, None, :], jnp.sin(angles)[:, None, :])


def contract_rows(first_operand, second_operand):
    return lax.dot_general(
        first_operand, second_operand, (((0,), (0,)), ((), ())), preferred_element_type=jnp.float32
    )


def times_transposed(first_operand, second_operand):
    return lax.dot_general(
        first_operand, second_operand, (((1,), (1,)), ((), ())), preferred_element_type=jnp.float32
    )


def simple_product(first_operand, second_operand):
    return jnp.dot(first_operand, second_operand, preferred_element_type=jnp.float32)


def masked_scores(query_block, key_seq, first_row):
    scale_factor = query_block.shape[-1] ** (-0.5)
    scores = (
        jnp.einsum("qhgd,khd->hgqk", query_block, key_seq, preferred_element_type=jnp.float32)
        * scale_factor
    )
    visible = (first_row + jnp.arange(query_block.shape[0]))[:, None] >= jnp.arange(
        key_seq.shape[0]
    )[None, :]
    return jnp.where(visible, scores, -1e30)


def attend_forward(query_block, key_seq, value_seq, first_row):
    scores = masked_scores(query_block, key_seq, first_row)
    highest = jnp.max(scores, axis=-1, keepdims=True)
    log_total = highest[..., 0] + jnp.log(jnp.sum(jnp.exp(scores - highest), axis=-1))
    weights = jnp.exp(scores - log_total[..., None]).astype(jnp.bfloat16)
    mixed_block = jnp.einsum(
        "hgqk,khd->qhgd", weights, value_seq, preferred_element_type=jnp.float32
    ).astype(jnp.bfloat16)
    return (mixed_block, log_total)


def attend_backward(
    query_block, key_seq, value_seq, mixed_block, slope_block, total_block, first_row
):
    scale_factor = query_block.shape[-1] ** (-0.5)
    scores = masked_scores(query_block, key_seq, first_row)
    weights = jnp.exp(scores - total_block[..., None])
    value_part = jnp.einsum(
        "hgqk,qhgd->khd",
        weights.astype(jnp.bfloat16),
        slope_block,
        preferred_element_type=jnp.float32,
    )
    weight_slope = jnp.einsum(
        "qhgd,khd->hgqk", slope_block, value_seq, preferred_element_type=jnp.float32
    )
    centre = jnp.transpose(
        jnp.sum(slope_block.astype(jnp.float32) * mixed_block.astype(jnp.float32), axis=-1),
        (1, 2, 0),
    )
    score_slope = (weights * (weight_slope - centre[..., None])).astype(jnp.bfloat16)
    query_part = (
        jnp.einsum("hgqk,khd->qhgd", score_slope, key_seq, preferred_element_type=jnp.float32)
        * scale_factor
    )
    key_part = (
        jnp.einsum("hgqk,qhgd->khd", score_slope, query_block, preferred_element_type=jnp.float32)
        * scale_factor
    )
    return (query_part, key_part, value_part)


def head_norm_back(turn_slope, cosine, sine, unit_values, scale_values, gain_values):
    norm_slope = turn_slope * cosine - rotate_half(turn_slope) * sine
    gain_term = jnp.sum(norm_slope * unit_values, axis=(0, 1))
    unit_slope = norm_slope * gain_values
    raw_slope = (
        scale_values
        * (unit_slope - unit_values * jnp.mean(unit_slope * unit_values, axis=-1, keepdims=True))
    ).astype(jnp.bfloat16)
    return (raw_slope.reshape(raw_slope.shape[0], -1), gain_term)


def per_device(
    block_input,
    attention_gain,
    query_weight,
    key_matrix,
    value_matrix,
    query_gain,
    key_gain,
    output_weight,
    feed_gain,
    gate_weight,
    up_weight,
    down_weight,
    out_cotangent,
):
    local_rows = block_input.shape[0]
    grouped_rows = local_rows * lax.axis_size("tensor")
    head_size = query_gain.shape[0]
    query_heads = query_weight.shape[1] // head_size
    value_heads = key_matrix.shape[1] // head_size
    grouping_width = query_heads // value_heads
    sequences = grouped_rows // SEQUENCE_LENGTH
    block_rows = min(512, SEQUENCE_LENGTH)
    block_count = SEQUENCE_LENGTH // block_rows
    cosine, sine = rope_tables(
        (jnp.arange(grouped_rows) % SEQUENCE_LENGTH).astype(jnp.float32), head_size
    )
    gathered = (
        lax.all_gather(query_weight, "dp", axis=0, tiled=True),
        lax.all_gather(key_matrix, "dp", axis=0, tiled=True),
        lax.all_gather(value_matrix, "dp", axis=0, tiled=True),
        lax.all_gather(output_weight, "dp", axis=1, tiled=True),
        lax.all_gather(gate_weight, "dp", axis=0, tiled=True),
        lax.all_gather(up_weight, "dp", axis=0, tiled=True),
        lax.all_gather(down_weight, "dp", axis=1, tiled=True),
    )
    query_full, key_full, value_full, output_full, gate_full, up_full, down_full = gathered
    input_float = block_input.astype(jnp.float32)
    first_scale = row_scale(input_float)
    first_unit = input_float * first_scale
    mixer_local = (first_unit * attention_gain).astype(jnp.bfloat16)
    attention_output_rows = lax.all_gather(mixer_local, "tensor", axis=0, tiled=True)
    query_raw = simple_product(attention_output_rows, query_full).reshape(
        grouped_rows, query_heads, head_size
    )
    unnormed_key = simple_product(attention_output_rows, key_full).reshape(
        grouped_rows, value_heads, head_size
    )
    value_token_rows = simple_product(attention_output_rows, value_full).astype(jnp.bfloat16)
    query_scale = row_scale(query_raw)
    query_unit = query_raw * query_scale
    query_normed = query_unit * query_gain
    rotated_query = (query_normed * cosine + rotate_half(query_normed) * sine).astype(jnp.bfloat16)
    key_norm_scale = row_scale(unnormed_key)
    normalized_key = unnormed_key * key_norm_scale
    key_normed = normalized_key * key_gain
    rotated_key = (key_normed * cosine + rotate_half(key_normed) * sine).astype(jnp.bfloat16)
    query_sequences = rotated_query.reshape(
        sequences, SEQUENCE_LENGTH, value_heads, grouping_width, head_size
    )
    key_sequences = rotated_key.reshape(sequences, SEQUENCE_LENGTH, value_heads, head_size)
    value_sequences = value_token_rows.reshape(sequences, SEQUENCE_LENGTH, value_heads, head_size)

    def forward_sequence(operands):
        query_seq, key_seq, value_seq = operands
        mixed_parts = []
        total_parts = []
        for block_index in range(block_count):
            first_row = block_index * block_rows
            mixed_block, log_total = attend_forward(
                query_seq[first_row : first_row + block_rows], key_seq, value_seq, first_row
            )
            mixed_parts.append(mixed_block)
            total_parts.append(log_total)
        return (jnp.concatenate(mixed_parts, axis=0), jnp.concatenate(total_parts, axis=-1))

    mixed_seqs, totals = lax.map(
        forward_sequence, (query_sequences, key_sequences, value_sequences)
    )
    mixed_rows = mixed_seqs.reshape(grouped_rows, query_heads * head_size)
    attention_sum = lax.psum_scatter(
        simple_product(
            lax.slice_in_dim(mixed_rows, 0, local_rows * lax.axis_size("tensor"), axis=0),
            output_full,
        ),
        "tensor",
        scatter_dimension=0,
        tiled=True,
    )
    hidden_state = input_float + attention_sum
    second_scale = row_scale(hidden_state)
    second_unit = hidden_state * second_scale
    feed_local = (second_unit * feed_gain).astype(jnp.bfloat16)
    feed_rows = lax.all_gather(feed_local, "tensor", axis=0, tiled=True)
    gate_values = simple_product(feed_rows, gate_full)
    up_values = simple_product(feed_rows, up_full)
    gate_sigmoid = jax.nn.sigmoid(gate_values)
    hidden_rows = (gate_values * gate_sigmoid * up_values).astype(jnp.bfloat16)
    feed_sum = lax.psum_scatter(
        simple_product(
            lax.slice_in_dim(hidden_rows, 0, local_rows * lax.axis_size("tensor"), axis=0),
            down_full,
        ).astype(jnp.bfloat16),
        "tensor",
        scatter_dimension=0,
        tiled=True,
    ).astype(jnp.float32)
    block_output = (hidden_state + feed_sum).astype(jnp.bfloat16)
    regathered = (
        lax.all_gather(query_weight, "dp", axis=0, tiled=True),
        lax.all_gather(key_matrix, "dp", axis=0, tiled=True),
        lax.all_gather(value_matrix, "dp", axis=0, tiled=True),
        lax.all_gather(output_weight, "dp", axis=1, tiled=True),
        lax.all_gather(gate_weight, "dp", axis=0, tiled=True),
        lax.all_gather(up_weight, "dp", axis=0, tiled=True),
        lax.all_gather(down_weight, "dp", axis=1, tiled=True),
    )
    query_back, key_back, value_back, output_back, gate_back, up_back, down_back = regathered
    cotangent_rows = lax.all_gather(out_cotangent, "tensor", axis=0, tiled=True)
    hidden_slope = times_transposed(cotangent_rows, down_back)
    down_grad = contract_rows(hidden_rows, cotangent_rows)
    gate_slope = (
        hidden_slope * up_values * gate_sigmoid * (1.0 + gate_values * (1.0 - gate_sigmoid))
    ).astype(jnp.bfloat16)
    up_slope = (hidden_slope * gate_values * gate_sigmoid).astype(jnp.bfloat16)
    gate_grad = contract_rows(feed_rows, gate_slope)
    up_grad = contract_rows(feed_rows, up_slope)
    gate_part = lax.slice_in_dim(gate_slope, 0, local_rows * lax.axis_size("tensor"), axis=0)
    up_part = lax.slice_in_dim(up_slope, 0, local_rows * lax.axis_size("tensor"), axis=0)
    feed_back = lax.psum_scatter(
        times_transposed(gate_part, gate_back) + times_transposed(up_part, up_back),
        "tensor",
        scatter_dimension=0,
        tiled=True,
    )
    feed_gain_term = jnp.sum(feed_back * second_unit, axis=0)
    feed_unit_slope = feed_back * feed_gain
    state_slope = out_cotangent.astype(jnp.float32) + second_scale * (
        feed_unit_slope
        - second_unit * jnp.mean(feed_unit_slope * second_unit, axis=-1, keepdims=True)
    )
    state_rounded = state_slope.astype(jnp.bfloat16)
    state_rows = lax.all_gather(state_rounded, "tensor", axis=0, tiled=True)
    mixed_gradient = times_transposed(state_rows, output_back).astype(jnp.bfloat16)
    output_grad = contract_rows(mixed_rows, state_rows)
    gradient_sequences = mixed_gradient.reshape(
        sequences, SEQUENCE_LENGTH, value_heads, grouping_width, head_size
    )

    def backward_sequence(operands):
        query_seq, key_seq, value_seq, mixed_seq, slope_seq, total_seq = operands
        key_total = jnp.zeros(key_seq.shape, jnp.float32)
        value_total = jnp.zeros(value_seq.shape, jnp.float32)
        query_parts = []
        for block_index in range(block_count):
            first_row = block_index * block_rows
            last_row = first_row + block_rows
            query_part, key_part, value_part = attend_backward(
                query_seq[first_row:last_row],
                key_seq,
                value_seq,
                mixed_seq[first_row:last_row],
                slope_seq[first_row:last_row],
                total_seq[..., first_row:last_row],
                first_row,
            )
            query_parts.append(query_part)
            key_total = key_total + key_part
            value_total = value_total + value_part
        return (jnp.concatenate(query_parts, axis=0), key_total, value_total.astype(jnp.bfloat16))

    query_slope, key_rows_gradient, value_rows_gradient = lax.map(
        backward_sequence,
        (query_sequences, key_sequences, value_sequences, mixed_seqs, gradient_sequences, totals),
    )
    query_raw_slope, query_gain_term = head_norm_back(
        query_slope.reshape(grouped_rows, query_heads, head_size),
        cosine,
        sine,
        query_unit,
        query_scale,
        query_gain,
    )
    unnormed_key_gradient, key_gain_term = head_norm_back(
        key_rows_gradient.reshape(grouped_rows, value_heads, head_size),
        cosine,
        sine,
        normalized_key,
        key_norm_scale,
        key_gain,
    )
    value_gradient_rows = value_rows_gradient.reshape(grouped_rows, value_heads * head_size)
    query_grad = contract_rows(attention_output_rows, query_raw_slope)
    key_grad = contract_rows(attention_output_rows, unnormed_key_gradient)
    value_grad = contract_rows(attention_output_rows, value_gradient_rows)
    query_part = lax.slice_in_dim(query_raw_slope, 0, local_rows * lax.axis_size("tensor"), axis=0)
    key_part = lax.slice_in_dim(
        unnormed_key_gradient, 0, local_rows * lax.axis_size("tensor"), axis=0
    )
    value_part = lax.slice_in_dim(
        value_gradient_rows, 0, local_rows * lax.axis_size("tensor"), axis=0
    )
    mixer_back = lax.psum_scatter(
        (
            times_transposed(query_part, query_back)
            + times_transposed(key_part, key_back)
            + times_transposed(value_part, value_back)
        ).astype(jnp.bfloat16),
        "tensor",
        scatter_dimension=0,
        tiled=True,
    ).astype(jnp.float32)
    attention_gain_term = jnp.sum(mixer_back * first_unit, axis=0)
    mixer_unit_slope = mixer_back * attention_gain
    input_gradient = (
        state_slope
        + first_scale
        * (
            mixer_unit_slope
            - first_unit * jnp.mean(mixer_unit_slope * first_unit, axis=-1, keepdims=True)
        )
    ).astype(jnp.bfloat16)
    weight_totals = (
        lax.psum_scatter(
            query_grad.astype(jnp.bfloat16), "dp", scatter_dimension=0, tiled=True
        ).astype(jnp.float32),
        lax.psum_scatter(
            key_grad.astype(jnp.bfloat16), "dp", scatter_dimension=0, tiled=True
        ).astype(jnp.float32),
        lax.psum_scatter(
            value_grad.astype(jnp.bfloat16), "dp", scatter_dimension=0, tiled=True
        ).astype(jnp.float32),
        lax.psum_scatter(
            output_grad.astype(jnp.bfloat16), "dp", scatter_dimension=1, tiled=True
        ).astype(jnp.float32),
        lax.psum_scatter(
            gate_grad.astype(jnp.bfloat16), "dp", scatter_dimension=0, tiled=True
        ).astype(jnp.float32),
        lax.psum_scatter(
            up_grad.astype(jnp.bfloat16), "dp", scatter_dimension=0, tiled=True
        ).astype(jnp.float32),
        lax.psum_scatter(
            down_grad.astype(jnp.bfloat16), "dp", scatter_dimension=1, tiled=True
        ).astype(jnp.float32),
    )
    gain_totals = lax.psum(
        (attention_gain_term, feed_gain_term, query_gain_term, key_gain_term), ("dp", "tensor")
    )
    return (
        block_output,
        input_gradient,
        gain_totals[0],
        weight_totals[0],
        weight_totals[1],
        weight_totals[2],
        gain_totals[2],
        gain_totals[3],
        weight_totals[3],
        gain_totals[1],
        weight_totals[4],
        weight_totals[5],
        weight_totals[6],
    )


def solution(mesh):
    in_specs = (
        P(("dp", "tensor"), None),
        P(),
        P("dp", "tensor"),
        P("dp", "tensor"),
        P("dp", "tensor"),
        P(),
        P(),
        P("tensor", "dp"),
        P(),
        P("dp", "tensor"),
        P("dp", "tensor"),
        P("tensor", "dp"),
        P(("dp", "tensor"), None),
    )
    out_specs = (
        P(("dp", "tensor"), None),
        P(("dp", "tensor"), None),
        P(),
        P("dp", "tensor"),
        P("dp", "tensor"),
        P("dp", "tensor"),
        P(),
        P(),
        P("tensor", "dp"),
        P(),
        P("dp", "tensor"),
        P("dp", "tensor"),
        P("tensor", "dp"),
    )
    return jax.shard_map(
        per_device, mesh=mesh, in_specs=in_specs, out_specs=out_specs, check_vma=False
    )
```

profile of v0, /device:TPU:0, one launch (start us, length us, event | category | flops | bytes accessed | tf_op | source)
XLA Modules:
  0.0 1226.1 jit_solution(7663798207786850853)
XLA Ops:
  17.2 17.3 %all-gather.16.cloned.1.call-done = bf16[2048,256]{1,0:T(8,128)(2,1)} async-done(((bf16[256,256]{1,0:T(8,128)(2,1)}), bf16[2048,256]{1,0:T(8,128)(2,1)}) %all-gather.16.cloned.1.call-update) | async-done | bytes 1048592 | tf_op jit(solution)/shard_map/all_gather | solution.py:138
  34.6 54.6 %all-gather.12.cloned.1.call-done = bf16[1024,2048]{1,0:T(8,128)(2,1)} async-done(((bf16[256,2048]{1,0:T(8,128)(2,1)}), bf16[1024,2048]{1,0:T(8,128)(2,1)}) %all-gather.12.cloned.1.call-update) | async-done | bytes 4194320 | tf_op jit(solution)/shard_map/all_gather | solution.py:150
  94.4 25.6 %all-gather.18.cloned.1.call-done = bf16[2048,512]{1,0:T(8,128)(2,1)} async-done(((bf16[256,512]{1,0:T(8,128)(2,1)}), bf16[2048,512]{1,0:T(8,128)(2,1)}) %all-gather.18.cloned.1.call-update) | async-done | bytes 2097168 | tf_op jit(solution)/shard_map/all_gather | solution.py:137
  155.8 19.0 %all-gather.20.cloned.1.call-done = bf16[512,2048]{1,0:T(8,128)(2,1)} async-done(((bf16[512,256]{1,0:T(8,128)(2,1)}), bf16[512,2048]{1,0:T(8,128)(2,1)}) %all-gather.20.cloned.1.call-update) | async-done | bytes 2097168 | tf_op jit(solution)/shard_map/all_gather | solution.py:140
  182.9 84.7 %reduce-scatter.12.cloned.1.call-done = f32[256,2048]{1,0:T(8,128)} async-done(((f32[1024,2048]{1,0:T(8,128)}), f32[256,2048]{1,0:T(8,128)}) %reduce-scatter.12.cloned.1.call-update) | async-done | bytes 2097168 | tf_op jit(solution)/shard_map/reduce_scatter | solution.py:189
  272.9 61.1 %all-gather.24.cloned.1.call-done = bf16[2048,1536]{1,0:T(8,128)(2,1)} async-done(((bf16[256,1536]{1,0:T(8,128)(2,1)}), bf16[2048,1536]{1,0:T(8,128)(2,1)}) %all-gather.24.cloned.1.call-update) | async-done | bytes 6291472 | tf_op jit(solution)/shard_map/all_gather | solution.py:141
  334.0 53.7 %all-gather.22.cloned.1.call-done = bf16[1024,2048]{1,0:T(8,128)(2,1)} async-done(((bf16[256,2048]{1,0:T(8,128)(2,1)}), bf16[1024,2048]{1,0:T(8,128)(2,1)}) %all-gather.22.cloned.1.call-update) | async-done | bytes 4194320 | tf_op jit(solution)/shard_map/all_gather | solution.py:202
  387.6 11.9 fusion.55
  399.5 54.5 %all-gather.26.cloned.1.call-done = bf16[2048,1536]{1,0:T(8,128)(2,1)} async-done(((bf16[256,1536]{1,0:T(8,128)(2,1)}), bf16[2048,1536]{1,0:T(8,128)(2,1)}) %all-gather.26.cloned.1.call-update) | async-done | bytes 6291472 | tf_op jit(solution)/shard_map/all_gather | solution.py:142
  454.0 11.7 fusion.56
  465.8 41.2 %all-gather.30.cloned.1.call-done = bf16[1024,2048]{1,0:T(8,128)(2,1)} async-done(((bf16[256,2048]{1,0:T(8,128)(2,1)}), bf16[1024,2048]{1,0:T(8,128)(2,1)}) %all-gather.30.cloned.1.call-update) | async-done | bytes 4194320 | tf_op jit(solution)/shard_map/all_gather | solution.py:227
  506.9 66.8 %all-gather.28.cloned.1.call-done = bf16[1536,2048]{1,0:T(8,128)(2,1)} async-done(((bf16[1536,256]{1,0:T(8,128)(2,1)}), bf16[1536,2048]{1,0:T(8,128)(2,1)}) %all-gather.28.cloned.1.call-update) | async-done | bytes 6291472 | tf_op jit(solution)/shard_map/all_gather | solution.py:143
  573.7 15.9 %multiply_convert_fusion = (bf16[1024,1536]{1,0:T(8,128)(2,1)S(1)}, bf16[1024,1536]{1,0:T(8,128)(2,1)S(1)}, bf16[1024,1536]{1,0:T(8,128)(2,1)}) fusion(f32[1024,1536]{1,0:T(8,128)} %fusion.55, f32[1024,1536]{1,0:T(8,128)} %fusion.56, bf16[1024,2048]{1,0:T(8,128)(2,1)} %all-gather.30.cloned.1.call-done, bf16[1536,2048]{1,0:T(8,128)(2,1)} %all-gather.28.cloned.1.call-done), kind=kOutput, calls=%fused_computation.18 | convolution fusion | flops 6467616768 | bytes 32505856 | tf_op jit(solution)/shard_map/dot_general | solution.py:35
  610.2 84.6 %reduce-scatter.16.cloned.1.call-done = f32[256,2048]{1,0:T(8,128)} async-done(((f32[1024,2048]{1,0:T(8,128)}), f32[256,2048]{1,0:T(8,128)}) %reduce-scatter.16.cloned.1.call-update) | async-done | bytes 2097168 | tf_op jit(solution)/shard_map/reduce_scatter | solution.py:238
  733.5 18.1 %all-gather.32.cloned.1.call-done = bf16[1024,2048]{1,0:T(8,128)(2,1)} async-done(((bf16[256,2048]{1,0:T(8,128)(2,1)}), bf16[1024,2048]{1,0:T(8,128)(2,1)}) %all-gather.32.cloned.1.call-update) | async-done | bytes 4194320 | tf_op jit(solution)/shard_map/all_gather | solution.py:251
  848.5 45.3 %reduce-scatter.30.cloned.1.call-done = bf16[256,1536]{1,0:T(8,128)(2,1)} async-done(((bf16[2048,1536]{1,0:T(8,128)(2,1)}), bf16[256,1536]{1,0:T(8,128)(2,1)}) %reduce-scatter.30.cloned.1.call-update) | async-done | bytes 786448 | tf_op jit(solution)/shard_map/reduce_scatter | solution.py:347
  896.3 67.9 %reduce-scatter.32.cloned.1.call-done = bf16[1536,256]{1,0:T(8,128)(2,1)} async-done(((bf16[1536,2048]{1,0:T(8,128)(2,1)}), bf16[1536,256]{1,0:T(8,128)(2,1)}) %reduce-scatter.32.cloned.1.call-update) | async-done | bytes 786448 | tf_op jit(solution)/shard_map/reduce_scatter | solution.py:350
  966.6 30.8 %reduce-scatter.24.cloned.1.call-done = bf16[256,256]{1,0:T(8,128)(2,1)} async-done(((bf16[2048,256]{1,0:T(8,128)(2,1)}), bf16[256,256]{1,0:T(8,128)(2,1)}) %reduce-scatter.24.cloned.1.call-update) | async-done | bytes 131088 | tf_op jit(solution)/shard_map/reduce_scatter | solution.py:338
  999.0 31.4 %reduce-scatter.22.cloned.1.call-done = bf16[256,256]{1,0:T(8,128)(2,1)} async-done(((bf16[2048,256]{1,0:T(8,128)(2,1)}), bf16[256,256]{1,0:T(8,128)(2,1)}) %reduce-scatter.22.cloned.1.call-update) | async-done | bytes 131088 | tf_op jit(solution)/shard_map/reduce_scatter | solution.py:335
  1032.1 34.9 %reduce-scatter.26.cloned.1.call-done = bf16[512,256]{1,0:T(8,128)(2,1)} async-done(((bf16[512,2048]{1,0:T(8,128)(2,1)}), bf16[512,256]{1,0:T(8,128)(2,1)}) %reduce-scatter.26.cloned.1.call-update) | async-done | bytes 262160 | tf_op jit(solution)/shard_map/reduce_scatter | solution.py:341
  1068.7 35.1 %reduce-scatter.20.cloned.1.call-done = bf16[256,512]{1,0:T(8,128)(2,1)} async-done(((bf16[2048,512]{1,0:T(8,128)(2,1)}), bf16[256,512]{1,0:T(8,128)(2,1)}) %reduce-scatter.20.cloned.1.call-update) | async-done | bytes 262160 | tf_op jit(solution)/shard_map/reduce_scatter | solution.py:332
  1105.6 52.4 %reduce-scatter.18.cloned.1.call-done = bf16[256,2048]{1,0:T(8,128)(2,1)} async-done(((bf16[1024,2048]{1,0:T(8,128)(2,1)}), bf16[256,2048]{1,0:T(8,128)(2,1)}) %reduce-scatter.18.cloned.1.call-update) | async-done | bytes 1048592 | tf_op jit(solution)/shard_map/reduce_scatter | solution.py:311
  1160.0 40.1 %all-reduce = (f32[2048]{0:T(1024)}, f32[128]{0:T(128)}, f32[128]{0:T(128)}, f32[2048]{0:T(1024)}) all-reduce(f32[2048]{0:T(1024)S(1)} %get-tuple-element.53, f32[128]{0:T(128)S(1)} %reduce_sum.170, f32[128]{0:T(128)S(1)} %get-tuple-element.65, f32[2048]{0:T(1024)S(1)} %get-tuple-element.51), channel_id=1, replica_groups=mesh['dp'=8,'tensor'=4] {'dp','tensor'}, use_global_device_ids=true, to_apply=%region_19.20 | all-reduce | flops 4352 | bytes 34816 | tf_op jit(solution)/shard_map/psum | solution.py:354
  1200.1 13.7 %reduce-scatter.14.cloned.1.call-done = bf16[256,2048]{1,0:T(8,128)(2,1)} async-done(((bf16[1024,2048]{1,0:T(8,128)(2,1)}), bf16[256,2048]{1,0:T(8,128)(2,1)}) %reduce-scatter.14.cloned.1.call-update) | async-done | bytes 1048592 | tf_op jit(solution)/shard_map/reduce_scatter | solution.py:207
  (280 shorter events, 237.9 us)
Async XLA Ops:
  7.2 27.4 %all-gather.16.cloned.1.call-start = ((), (), s32[]{:S(2)}) async-start(), calls=%async_computation.13 | async-start | bytes 1179648 | tf_op jit(solution)/shard_map/all_gather | solution.py:138
  7.9 81.3 %all-gather.12.cloned.1.call-start = ((), (), s32[]{:S(2)}) async-start(), calls=%async_computation.11 | async-start | bytes 5242880 | tf_op jit(solution)/shard_map/all_gather | solution.py:150
  12.0 108.0 %all-gather.18.cloned.1.call-start = ((), (), s32[]{:S(2)}) async-start(), calls=%async_computation.14 | async-start | bytes 2359296 | tf_op jit(solution)/shard_map/all_gather | solution.py:137
  12.8 130.4 %all-gather.14.cloned.1.call-start = ((), (), s32[]{:S(2)}) async-start(), calls=%async_computation.12 | async-start | bytes 1179648 | tf_op jit(solution)/shard_map/all_gather | solution.py:139
  13.3 161.5 %all-gather.20.cloned.1.call-start = ((), (), s32[]{:S(2)}) async-start(), calls=%async_computation.15 | async-start | bytes 2359296 | tf_op jit(solution)/shard_map/all_gather | solution.py:140
  13.9 253.7 %reduce-scatter.12.cloned.1.call-start = ((), (), s32[]{:S(2)}) async-start(), calls=%async_computation.16 | async-start | bytes 10485760 | tf_op jit(solution)/shard_map/reduce_scatter | solution.py:189
  182.1 151.8 %all-gather.24.cloned.1.call-start = ((), (), s32[]{:S(2)}) async-start(), calls=%async_computation.18 | async-start | bytes 7077888 | tf_op jit(solution)/shard_map/all_gather | solution.py:141
  182.9 204.8 %all-gather.22.cloned.1.call-start = ((), (), s32[]{:S(2)}) async-start(), calls=%async_computation.17 | async-start | bytes 5242880 | tf_op jit(solution)/shard_map/all_gather | solution.py:202
  270.8 183.2 %all-gather.26.cloned.1.call-start = ((), (), s32[]{:S(2)}) async-start(), calls=%async_computation.19 | async-start | bytes 7077888 | tf_op jit(solution)/shard_map/all_gather | solution.py:142
  271.5 235.4 %all-gather.30.cloned.1.call-start = ((), (), s32[]{:S(2)}) async-start(), calls=%async_computation.22 | async-start | bytes 5242880 | tf_op jit(solution)/shard_map/all_gather | solution.py:227
  272.1 301.6 %all-gather.28.cloned.1.call-start = ((), (), s32[]{:S(2)}) async-start(), calls=%async_computation.20 | async-start | bytes 7077888 | tf_op jit(solution)/shard_map/all_gather | solution.py:143
  272.8 422.0 %reduce-scatter.16.cloned.1.call-start = ((), (), s32[]{:S(2)}) async-start(), calls=%async_computation.23 | async-start | bytes 10485760 | tf_op jit(solution)/shard_map/reduce_scatter | solution.py:238
  610.2 141.4 %all-gather.32.cloned.1.call-start = ((), (), s32[]{:S(2)}) async-start(), calls=%async_computation.24 | async-start | bytes 5242880 | tf_op jit(solution)/shard_map/all_gather | solution.py:251
  698.8 147.2 %reduce-scatter.28.cloned.1.call-start = ((), (), s32[]{:S(2)}) async-start(), calls=%async_computation.30 | async-start | bytes 7077888 | tf_op jit(solution)/shard_map/reduce_scatter | solution.py:344
  710.3 183.5 %reduce-scatter.30.cloned.1.call-start = ((), (), s32[]{:S(2)}) async-start(), calls=%async_computation.31 | async-start | bytes 7077888 | tf_op jit(solution)/shard_map/reduce_scatter | solution.py:347
  721.9 242.3 %reduce-scatter.32.cloned.1.call-start = ((), (), s32[]{:S(2)}) async-start(), calls=%async_computation.32 | async-start | bytes 7077888 | tf_op jit(solution)/shard_map/reduce_scatter | solution.py:350
  733.2 264.2 %reduce-scatter.24.cloned.1.call-start = ((), (), s32[]{:S(2)}) async-start(), calls=%async_computation.28 | async-start | bytes 1179648 | tf_op jit(solution)/shard_map/reduce_scatter | solution.py:338
  786.4 244.0 %reduce-scatter.22.cloned.1.call-start = ((), (), s32[]{:S(2)}) async-start(), calls=%async_computation.27 | async-start | bytes 1179648 | tf_op jit(solution)/shard_map/reduce_scatter | solution.py:335
  798.2 268.7 %reduce-scatter.26.cloned.1.call-start = ((), (), s32[]{:S(2)}) async-start(), calls=%async_computation.29 | async-start | bytes 2359296 | tf_op jit(solution)/shard_map/reduce_scatter | solution.py:341
  804.6 299.2 %reduce-scatter.20.cloned.1.call-start = ((), (), s32[]{:S(2)}) async-start(), calls=%async_computation.26 | async-start | bytes 2359296 | tf_op jit(solution)/shard_map/reduce_scatter | solution.py:332
  825.8 332.1 %reduce-scatter.18.cloned.1.call-start = ((), (), s32[]{:S(2)}) async-start(), calls=%async_computation.25 | async-start | bytes 5242880 | tf_op jit(solution)/shard_map/reduce_scatter | solution.py:311
  834.4 379.4 %reduce-scatter.14.cloned.1.call-start = ((), (), s32[]{:S(2)}) async-start(), calls=%async_computation.21 | async-start | bytes 5242880 | tf_op jit(solution)/shard_map/reduce_scatter | solution.py:207
  845.9 312.0 %copy-start.6 = (bf16[256,2048]{1,0:T(8,128)(2,1)S(1)}, bf16[256,2048]{1,0:T(8,128)(2,1)}, u32[]{:S(2)}) copy-start(bf16[256,2048]{1,0:T(8,128)(2,1)} %param.13) | copy-start | bytes 3145732
  845.9 312.0 %copy-start.53 = (f32[2048]{0:T(1024)S(1)}, f32[2048]{0:T(1024)}, u32[]{:S(2)}) copy-start(f32[2048]{0:T(1024)} %param.14) | copy-start | bytes 24580
  (71 other events, 1454.6 us)
Sparse Core Ops, SparseCore 0:
  9.6 24.9 all-gather.15
  37.0 52.1 all-gather.11
  90.8 29.1 all-gather.17
  121.5 21.6 all-gather.13
  144.6 30.1 all-gather.19
  182.2 85.2 reduce-scatter.11
  269.2 64.7 all-gather.23
  336.4 51.2 all-gather.21
  389.3 64.6 all-gather.25
  455.7 51.2 all-gather.29
  508.5 65.1 all-gather.27
  610.3 84.4 reduce-scatter.15
  698.9 52.5 all-gather.31
  753.7 69.7 reduce-scatter.27
  825.6 68.1 reduce-scatter.29
  896.0 68.1 reduce-scatter.31
  966.3 31.0 reduce-scatter.23
  999.5 30.8 reduce-scatter.21
  1032.7 34.1 reduce-scatter.25
  1069.1 34.6 reduce-scatter.19
  1106.8 51.1 reduce-scatter.17
  1160.9 52.8 reduce-scatter.13
where the time goes:
time: 1240 us; the launch traced here: 1230 us
  waiting for transfers between devices  902 us (73%)
  matrix products  201 us (16%)
  other arithmetic  53.5 us (4%)
  blocking collectives  40.1 us (3%)
  between operations  16 us (1%)
    reduce_scatter x1, waiting for transfers between devices, per_device(): lax.psum_scatter(simple_product(lax.slice_in_dim(mixed_rows, 0, local_row...  84.7 us
    reduce_scatter x1, waiting for transfers between devices, per_device(): lax.psum_scatter(times_transposed(gate_part, gate_back) + times_transpose...  84.6 us
    reduce_scatter x1, waiting for transfers between devices, per_device(): lax.psum_scatter(down_grad.astype(jnp.bfloat16), 'dp', scatter_dimension=...  67.9 us
    all_gather x1, waiting for transfers between devices, per_device(): lax.all_gather(down_weight, 'dp', axis=1, tiled=True)  66.8 us
    all_gather x1, waiting for transfers between devices, per_device(): lax.all_gather(gate_weight, 'dp', axis=0, tiled=True)  61.1 us
    dot_general x7, matrix products, simple_product(): jnp.dot(first_operand, second_operand, preferred_element_type=jnp.float32)  55 us
    all_gather x1, waiting for transfers between devices, per_device(): lax.all_gather(mixer_local, 'tensor', axis=0, tiled=True)  54.6 us
    all_gather x1, waiting for transfers between devices, per_device(): lax.all_gather(up_weight, 'dp', axis=0, tiled=True)  54.5 us
  transfers between devices with their start and end apart: 22, of which 21 were waited for; matrix products, arithmetic and copies ran while one was open for 17% of the time, Pallas kernels for 0%

commit v1 on v0

--- a/solution.py
+++ b/solution.py
@@ -6,6 +6,27 @@
 SEQUENCE_LENGTH = 1024
 epsilon = 1e-06
 rope_base = 1000000.0
+
+
+def collect(shard, axis, dim):
+    size, here, span = (lax.axis_size(axis), lax.axis_index(axis), shard.shape[dim])
+    ahead = [(i, (i + 1) % size) for i in range(size)]
+    left = [(i, (i - 1) % size) for i in range(size)]
+    whole = jnp.zeros((*shard.shape[:dim], size * span, *shard.shape[dim + 1 :]), shard.dtype)
+    whole = lax.dynamic_update_slice_in_dim(whole, shard, here * span, axis=dim)
+    from_left = from_right = shard
+    half = size // 2
+    for lap in range(1, half + 1):
+        from_left = lax.ppermute(from_left, axis, ahead)
+        whole = lax.dynamic_update_slice_in_dim(
+            whole, from_left, (here - lap) % size * span, axis=dim
+        )
+        if lap < size - half:
+            from_right = lax.ppermute(from_right, axis, left)
+            whole = lax.dynamic_update_slice_in_dim(
+                whole, from_right, (here + lap) % size * span, axis=dim
+            )
+    return whole
 
 
 def row_scale(values):
@@ -147,7 +168,7 @@
     first_scale = row_scale(input_float)
     first_unit = input_float * first_scale
     mixer_local = (first_unit * attention_gain).astype(jnp.bfloat16)
-    attention_output_rows = lax.all_gather(mixer_local, "tensor", axis=0, tiled=True)
+    attention_output_rows = collect(mixer_local, "tensor", 0)
     query_raw = simple_product(attention_output_rows, query_full).reshape(
         grouped_rows, query_heads, head_size
     )

time: 1240 us -> 1180 us (0.952)
  waiting for transfers between devices: 902 us -> 836 us
    ppermute x0 -> x3, waiting for transfers between devices: none -> 59.7 us  [the longest x2 42.8 us: collect(): from_left = lax.ppermute(from_left, axis, ahead)]
    all_gather x1 -> x0, waiting for transfers between devices: 54.6 us -> none  [per_device(): lax.all_gather(mixer_local, 'tensor', axis=0, tiled=True)]
    all_gather x1, waiting for transfers between devices: 25.6 us -> 0.01 us  [per_device(): lax.all_gather(query_weight, 'dp', axis=0, tiled=True)]
    all_gather x1, waiting for transfers between devices: 19 us -> 0.02 us  [per_device(): lax.all_gather(output_weight, 'dp', axis=1, tiled=True)]
    all_gather x1, waiting for transfers between devices: 17.3 us -> 0.01 us  [per_device(): lax.all_gather(key_matrix, 'dp', axis=0, tiled=True)]
  transfers between devices with their start and end apart: 22 -> 24, of which waited for: 21 -> 19; matrix products, arithmetic and copies ran while one was open for 17% -> 18% of each run, Pallas kernels for 0% -> 0%
where the time goes in v1:
time: 1180 us; the launch traced here: 1170 us
  waiting for transfers between devices  836 us (71%)
  matrix products  206 us (17%)
  other arithmetic  53.1 us (4%)
  blocking collectives  40.1 us (3%)
  local copies, waits for them, and re-layouts  17.1 us (1%)
  between operations  16 us (1%)
    reduce_scatter x1, waiting for transfers between devices, per_device(): lax.psum_scatter(simple_product(lax.slice_in_dim(mixed_rows, 0, local_row...  86.4 us
    reduce_scatter x1, waiting for transfers between devices, per_device(): lax.psum_scatter(times_transposed(gate_part, gate_back) + times_transpose...  84.6 us
    reduce_scatter x1, waiting for transfers between devices, per_device(): lax.psum_scatter(down_grad.astype(jnp.bfloat16), 'dp', scatter_dimension=...  67.9 us
    all_gather x1, waiting for transfers between devices, per_device(): lax.all_gather(down_weight, 'dp', axis=1, tiled=True)  66.6 us
    all_gather x1, waiting for transfers between devices, per_device(): lax.all_gather(gate_weight, 'dp', axis=0, tiled=True)  60.9 us
    dot_general x7, matrix products, simple_product(): jnp.dot(first_operand, second_operand, preferred_element_type=jnp.float32)  56.3 us
    dot_general x7, matrix products, contract_rows(): lax.dot_general(first_operand, second_operand, (((0,), (0,)), ((), ())),...  55.7 us
    all_gather x1, waiting for transfers between devices, per_device(): lax.all_gather(up_weight, 'dp', axis=0, tiled=True)  54.5 us
  transfers between devices with their start and end apart: 24, of which 19 were waited for; matrix products, arithmetic and copies ran while one was open for 18% of the time, Pallas kernels for 0%

profile of v1, /device:TPU:0, one launch (start us, length us, event | category | flops | bytes accessed | tf_op | source)
XLA Modules:
  0.0 1174.8 jit_solution(12900673395106049549)
XLA Ops:
  19.3 24.0 %collective-permute-done = bf16[256,2048]{1,0:T(8,128)(2,1)S(1)} collective-permute-done((bf16[256,2048]{1,0:T(8,128)(2,1)}, bf16[256,2048]{1,0:T(8,128)(2,1)S(1)}, u32[]{:S(2)}, u32[]{:S(2)}) %collective-permute-start) | collective-permute-done | bytes 1048608 | tf_op jit(solution)/shard_map/ppermute | solution.py:20
  49.5 16.9 %collective-permute-done.1 = bf16[256,2048]{1,0:T(8,128)(2,1)} collective-permute-done((bf16[256,2048]{1,0:T(8,128)(2,1)}, bf16[256,2048]{1,0:T(8,128)(2,1)}, u32[]{:S(2)}, u32[]{:S(2)}) %collective-permute-start.1) | collective-permute-done | bytes 1048608 | tf_op jit(solution)/shard_map/ppermute | solution.py:25
  68.8 18.7 %collective-permute-done.2 = bf16[256,2048]{1,0:T(8,128)(2,1)} collective-permute-done((bf16[256,2048]{1,0:T(8,128)(2,1)S(1)}, bf16[256,2048]{1,0:T(8,128)(2,1)}, u32[]{:S(2)}, u32[]{:S(2)}) %collective-permute-start.2) | collective-permute-done | bytes 1048608 | tf_op jit(solution)/shard_map/ppermute | solution.py:20
  129.8 86.4 %reduce-scatter.12.cloned.1.call-done = f32[256,2048]{1,0:T(8,128)} async-done(((f32[1024,2048]{1,0:T(8,128)}), f32[256,2048]{1,0:T(8,128)}) %reduce-scatter.12.cloned.1.call-update) | async-done | bytes 2097168 | tf_op jit(solution)/shard_map/reduce_scatter | solution.py:210
  221.5 60.9 %all-gather.21.cloned.1.call-done = bf16[2048,1536]{1,0:T(8,128)(2,1)} async-done(((bf16[256,1536]{1,0:T(8,128)(2,1)}), bf16[2048,1536]{1,0:T(8,128)(2,1)}) %all-gather.21.cloned.1.call-update) | async-done | bytes 6291472 | tf_op jit(solution)/shard_map/all_gather | solution.py:162
  282.4 53.7 %all-gather.19.cloned.1.call-done = bf16[1024,2048]{1,0:T(8,128)(2,1)} async-done(((bf16[256,2048]{1,0:T(8,128)(2,1)}), bf16[1024,2048]{1,0:T(8,128)(2,1)}) %all-gather.19.cloned.1.call-update) | async-done | bytes 4194320 | tf_op jit(solution)/shard_map/all_gather | solution.py:223
  336.1 11.9 %fusion.56 = f32[1024,1536]{1,0:T(8,128)} fusion(bf16[1024,2048]{1,0:T(8,128)(2,1)} %all-gather.19.cloned.1.call-done, bf16[2048,1536]{1,0:T(8,128)(2,1)} %all-gather.21.cloned.1.call-done), kind=kOutput, calls=%fused_computation.142 | convolution fusion | flops 6442450944 | bytes 16777216 | tf_op jit(solution)/shard_map/dot_general | solution.py:62
  348.0 54.5 %all-gather.23.cloned.1.call-done = bf16[2048,1536]{1,0:T(8,128)(2,1)} async-done(((bf16[256,1536]{1,0:T(8,128)(2,1)}), bf16[2048,1536]{1,0:T(8,128)(2,1)}) %all-gather.23.cloned.1.call-update) | async-done | bytes 6291472 | tf_op jit(solution)/shard_map/all_gather | solution.py:163
  402.5 11.7 fusion.57
  414.1 41.4 %all-gather.27.cloned.1.call-done = bf16[1024,2048]{1,0:T(8,128)(2,1)} async-done(((bf16[256,2048]{1,0:T(8,128)(2,1)}), bf16[1024,2048]{1,0:T(8,128)(2,1)}) %all-gather.27.cloned.1.call-update) | async-done | bytes 4194320 | tf_op jit(solution)/shard_map/all_gather | solution.py:248
  455.6 66.6 %all-gather.25.cloned.1.call-done = bf16[1536,2048]{1,0:T(8,128)(2,1)} async-done(((bf16[1536,256]{1,0:T(8,128)(2,1)}), bf16[1536,2048]{1,0:T(8,128)(2,1)}) %all-gather.25.cloned.1.call-update) | async-done | bytes 6291472 | tf_op jit(solution)/shard_map/all_gather | solution.py:164
  522.2 15.9 %multiply_convert_fusion = (bf16[1024,1536]{1,0:T(8,128)(2,1)S(1)}, bf16[1024,1536]{1,0:T(8,128)(2,1)S(1)}, bf16[1024,1536]{1,0:T(8,128)(2,1)}) fusion(f32[1024,1536]{1,0:T(8,128)} %fusion.56, f32[1024,1536]{1,0:T(8,128)} %fusion.57, bf16[1024,2048]{1,0:T(8,128)(2,1)} %all-gather.27.cloned.1.call-done, bf16[1536,2048]{1,0:T(8,128)(2,1)} %all-gather.25.cloned.1.call-done), kind=kOutput, calls=%fused_computation.18 | convolution fusion | flops 6467616768 | bytes 32505856 | tf_op jit(solution)/shard_map/dot_general | solution.py:56
  558.8 84.6 %reduce-scatter.16.cloned.1.call-done = f32[256,2048]{1,0:T(8,128)} async-done(((f32[1024,2048]{1,0:T(8,128)}), f32[256,2048]{1,0:T(8,128)}) %reduce-scatter.16.cloned.1.call-update) | async-done | bytes 2097168 | tf_op jit(solution)/shard_map/reduce_scatter | solution.py:259
  647.4 11.5 convolution_convert_fusion.2
  682.1 18.0 %all-gather.29.cloned.1.call-done = bf16[1024,2048]{1,0:T(8,128)(2,1)} async-done(((bf16[256,2048]{1,0:T(8,128)(2,1)}), bf16[1024,2048]{1,0:T(8,128)(2,1)}) %all-gather.29.cloned.1.call-update) | async-done | bytes 4194320 | tf_op jit(solution)/shard_map/all_gather | solution.py:272
  803.0 39.6 %reduce-scatter.30.cloned.1.call-done = bf16[256,1536]{1,0:T(8,128)(2,1)} async-done(((bf16[2048,1536]{1,0:T(8,128)(2,1)}), bf16[256,1536]{1,0:T(8,128)(2,1)}) %reduce-scatter.30.cloned.1.call-update) | async-done | bytes 786448 | tf_op jit(solution)/shard_map/reduce_scatter | solution.py:368
  845.0 67.9 %reduce-scatter.32.cloned.1.call-done = bf16[1536,256]{1,0:T(8,128)(2,1)} async-done(((bf16[1536,2048]{1,0:T(8,128)(2,1)}), bf16[1536,256]{1,0:T(8,128)(2,1)}) %reduce-scatter.32.cloned.1.call-update) | async-done | bytes 786448 | tf_op jit(solution)/shard_map/reduce_scatter | solution.py:371
  915.3 30.8 %reduce-scatter.24.cloned.1.call-done = bf16[256,256]{1,0:T(8,128)(2,1)} async-done(((bf16[2048,256]{1,0:T(8,128)(2,1)}), bf16[256,256]{1,0:T(8,128)(2,1)}) %reduce-scatter.24.cloned.1.call-update) | async-done | bytes 131088 | tf_op jit(solution)/shard_map/reduce_scatter | solution.py:359
  947.7 31.3 %reduce-scatter.22.cloned.1.call-done = bf16[256,256]{1,0:T(8,128)(2,1)} async-done(((bf16[2048,256]{1,0:T(8,128)(2,1)}), bf16[256,256]{1,0:T(8,128)(2,1)}) %reduce-scatter.22.cloned.1.call-update) | async-done | bytes 131088 | tf_op jit(solution)/shard_map/reduce_scatter | solution.py:356
  980.7 34.8 %reduce-scatter.26.cloned.1.call-done = bf16[512,256]{1,0:T(8,128)(2,1)} async-done(((bf16[512,2048]{1,0:T(8,128)(2,1)}), bf16[512,256]{1,0:T(8,128)(2,1)}) %reduce-scatter.26.cloned.1.call-update) | async-done | bytes 262160 | tf_op jit(solution)/shard_map/reduce_scatter | solution.py:362
  1017.3 35.2 %reduce-scatter.20.cloned.1.call-done = bf16[256,512]{1,0:T(8,128)(2,1)} async-done(((bf16[2048,512]{1,0:T(8,128)(2,1)}), bf16[256,512]{1,0:T(8,128)(2,1)}) %reduce-scatter.20.cloned.1.call-update) | async-done | bytes 262160 | tf_op jit(solution)/shard_map/reduce_scatter | solution.py:353
  1054.3 52.3 %reduce-scatter.18.cloned.1.call-done = bf16[256,2048]{1,0:T(8,128)(2,1)} async-done(((bf16[1024,2048]{1,0:T(8,128)(2,1)}), bf16[256,2048]{1,0:T(8,128)(2,1)}) %reduce-scatter.18.cloned.1.call-update) | async-done | bytes 1048592 | tf_op jit(solution)/shard_map/reduce_scatter | solution.py:332
  1108.7 40.1 %all-reduce = (f32[2048]{0:T(1024)}, f32[128]{0:T(128)}, f32[128]{0:T(128)}, f32[2048]{0:T(1024)}) all-reduce(f32[2048]{0:T(1024)S(1)} %get-tuple-element.53, f32[128]{0:T(128)S(1)} %reduce_sum.170, f32[128]{0:T(128)S(1)} %get-tuple-element.65, f32[2048]{0:T(1024)S(1)} %get-tuple-element.51), channel_id=1, replica_groups=mesh['dp'=8,'tensor'=4] {'dp','tensor'}, use_global_device_ids=true, to_apply=%region_19.20 | all-reduce | flops 4352 | bytes 34816 | tf_op jit(solution)/shard_map/psum | solution.py:375
  1148.8 13.7 %reduce-scatter.14.cloned.1.call-done = bf16[256,2048]{1,0:T(8,128)(2,1)} async-done(((bf16[1024,2048]{1,0:T(8,128)(2,1)}), bf16[256,2048]{1,0:T(8,128)(2,1)}) %reduce-scatter.14.cloned.1.call-update) | async-done | bytes 1048592 | tf_op jit(solution)/shard_map/reduce_scatter | solution.py:228
  (278 shorter events, 236.3 us)
Async XLA Ops:
  7.2 82.6 %all-gather.13.cloned.1.call-start = ((), (), s32[]{:S(2)}) async-start(), calls=%async_computation.12 | async-start | bytes 1179648 | tf_op jit(solution)/shard_map/all_gather | solution.py:159
  7.9 87.6 %all-gather.11.cloned.1.call-start = ((), (), s32[]{:S(2)}) async-start(), calls=%async_computation.11 | async-start | bytes 1179648 | tf_op jit(solution)/shard_map/all_gather | solution.py:160
  8.7 91.7 %all-gather.15.cloned.1.call-start = ((), (), s32[]{:S(2)}) async-start(), calls=%async_computation.13 | async-start | bytes 2359296 | tf_op jit(solution)/shard_map/all_gather | solution.py:158
  9.4 112.0 %all-gather.17.cloned.1.call-start = ((), (), s32[]{:S(2)}) async-start(), calls=%async_computation.14 | async-start | bytes 2359296 | tf_op jit(solution)/shard_map/all_gather | solution.py:161
  15.2 28.1 %collective-permute-start = (bf16[256,2048]{1,0:T(8,128)(2,1)}, bf16[256,2048]{1,0:T(8,128)(2,1)S(1)}, u32[]{:S(2)}, u32[]{:S(2)}) collective-permute-start(bf16[256,2048]{1,0:T(8,128)(2,1)} %get-tuple-element.79), channel_id=1, source_target_pairs={{0,1},{1,2},{2,3},{3,0},{4,5},{5,6},{6,7},{7,4},{8,9},{9,10},{10,1... | collective-permute-start | bytes 3145736 | tf_op jit(solution)/shard_map/ppermute | solution.py:20
  18.2 48.2 %collective-permute-start.1 = (bf16[256,2048]{1,0:T(8,128)(2,1)}, bf16[256,2048]{1,0:T(8,128)(2,1)}, u32[]{:S(2)}, u32[]{:S(2)}) collective-permute-start(bf16[256,2048]{1,0:T(8,128)(2,1)} %get-tuple-element.79), channel_id=1, source_target_pairs={{0,3},{1,0},{2,1},{3,2},{4,7},{5,4},{6,5},{7,6},{8,11},{9,8},{10,9... | collective-permute-start | bytes 3145736 | tf_op jit(solution)/shard_map/ppermute | solution.py:25
  19.1 197.1 %reduce-scatter.12.cloned.1.call-start = ((), (), s32[]{:S(2)}) async-start(), calls=%async_computation.15 | async-start | bytes 10485760 | tf_op jit(solution)/shard_map/reduce_scatter | solution.py:210
  43.3 44.2 %collective-permute-start.2 = (bf16[256,2048]{1,0:T(8,128)(2,1)S(1)}, bf16[256,2048]{1,0:T(8,128)(2,1)}, u32[]{:S(2)}, u32[]{:S(2)}) collective-permute-start(bf16[256,2048]{1,0:T(8,128)(2,1)S(1)} %collective-permute-done), channel_id=1, source_target_pairs={{0,1},{1,2},{2,3},{3,0},{4,5},{5,6},{6,7},{7,4},{8,9},{9,10},{10,1... | collective-permute-start | bytes 3145736 | tf_op jit(solution)/shard_map/ppermute | solution.py:20
  129.2 153.3 %all-gather.21.cloned.1.call-start = ((), (), s32[]{:S(2)}) async-start(), calls=%async_computation.17 | async-start | bytes 7077888 | tf_op jit(solution)/shard_map/all_gather | solution.py:162
  129.8 206.4 %all-gather.19.cloned.1.call-start = ((), (), s32[]{:S(2)}) async-start(), calls=%async_computation.16 | async-start | bytes 5242880 | tf_op jit(solution)/shard_map/all_gather | solution.py:223
  219.4 183.1 %all-gather.23.cloned.1.call-start = ((), (), s32[]{:S(2)}) async-start(), calls=%async_computation.18 | async-start | bytes 7077888 | tf_op jit(solution)/shard_map/all_gather | solution.py:163
  220.2 235.4 %all-gather.27.cloned.1.call-start = ((), (), s32[]{:S(2)}) async-start(), calls=%async_computation.21 | async-start | bytes 5242880 | tf_op jit(solution)/shard_map/all_gather | solution.py:248
  220.9 301.3 %all-gather.25.cloned.1.call-start = ((), (), s32[]{:S(2)}) async-start(), calls=%async_computation.19 | async-start | bytes 7077888 | tf_op jit(solution)/shard_map/all_gather | solution.py:164
  221.5 421.8 %reduce-scatter.16.cloned.1.call-start = ((), (), s32[]{:S(2)}) async-start(), calls=%async_computation.22 | async-start | bytes 10485760 | tf_op jit(solution)/shard_map/reduce_scatter | solution.py:259
  558.7 141.4 %all-gather.29.cloned.1.call-start = ((), (), s32[]{:S(2)}) async-start(), calls=%async_computation.23 | async-start | bytes 5242880 | tf_op jit(solution)/shard_map/all_gather | solution.py:272
  647.3 153.1 %reduce-scatter.28.cloned.1.call-start = ((), (), s32[]{:S(2)}) async-start(), calls=%async_computation.29 | async-start | bytes 7077888 | tf_op jit(solution)/shard_map/reduce_scatter | solution.py:365
  659.0 183.6 %reduce-scatter.30.cloned.1.call-start = ((), (), s32[]{:S(2)}) async-start(), calls=%async_computation.30 | async-start | bytes 7077888 | tf_op jit(solution)/shard_map/reduce_scatter | solution.py:368
  670.5 242.4 %reduce-scatter.32.cloned.1.call-start = ((), (), s32[]{:S(2)}) async-start(), calls=%async_computation.31 | async-start | bytes 7077888 | tf_op jit(solution)/shard_map/reduce_scatter | solution.py:371
  681.9 264.3 %reduce-scatter.24.cloned.1.call-start = ((), (), s32[]{:S(2)}) async-start(), calls=%async_computation.27 | async-start | bytes 1179648 | tf_op jit(solution)/shard_map/reduce_scatter | solution.py:359
  737.3 241.8 %reduce-scatter.22.cloned.1.call-start = ((), (), s32[]{:S(2)}) async-start(), calls=%async_computation.26 | async-start | bytes 1179648 | tf_op jit(solution)/shard_map/reduce_scatter | solution.py:356
  750.6 265.0 %reduce-scatter.26.cloned.1.call-start = ((), (), s32[]{:S(2)}) async-start(), calls=%async_computation.28 | async-start | bytes 2359296 | tf_op jit(solution)/shard_map/reduce_scatter | solution.py:362
  756.9 295.6 %reduce-scatter.20.cloned.1.call-start = ((), (), s32[]{:S(2)}) async-start(), calls=%async_computation.25 | async-start | bytes 2359296 | tf_op jit(solution)/shard_map/reduce_scatter | solution.py:353
  780.2 326.4 %reduce-scatter.18.cloned.1.call-start = ((), (), s32[]{:S(2)}) async-start(), calls=%async_computation.24 | async-start | bytes 5242880 | tf_op jit(solution)/shard_map/reduce_scatter | solution.py:332
  788.8 373.6 %reduce-scatter.14.cloned.1.call-start = ((), (), s32[]{:S(2)}) async-start(), calls=%async_computation.20 | async-start | bytes 5242880 | tf_op jit(solution)/shard_map/reduce_scatter | solution.py:228
  (69 other events, 1508.4 us)
Sparse Core Ops, SparseCore 0:
  9.6 24.9 all-gather.12
  36.2 21.8 all-gather.10
  59.7 28.7 all-gather.14
  89.9 30.0 all-gather.16
  129.3 86.8 reduce-scatter.11
  217.7 64.6 all-gather.20
  284.9 51.2 all-gather.18
  337.8 64.6 all-gather.22
  404.3 51.2 all-gather.26
  457.0 65.1 all-gather.24
  558.8 84.4 reduce-scatter.15
  647.5 52.5 all-gather.28
  702.4 69.7 reduce-scatter.27
  774.3 68.1 reduce-scatter.29
  844.7 68.1 reduce-scatter.31
  915.0 31.0 reduce-scatter.23
  948.2 30.7 reduce-scatter.21
  981.2 34.2 reduce-scatter.25
  1017.8 34.6 reduce-scatter.19
  1055.4 51.2 reduce-scatter.17
  1109.6 52.8 reduce-scatter.13
